TPU v7x, 32 devices: a whole 2x2x4 slice. The times are simulated.
32 devices in a mesh: seq: 8 (over z, y), head: 4 (over x, core).
Axes of the slice: x: 2, y: 2, z: 4, core: 2. Of those that a mesh axis runs over, the one named last changes fastest.
Arguments:
- queries: bfloat16 [6144, 4096], P(('seq', 'head')), may hold values from -6 to 6
- key_rows: bfloat16 [6144, 4096], P(('seq', 'head')), may hold values from -6 to 6
- values: bfloat16 [6144, 4096], P(('seq', 'head')), may hold values from -6 to 6
- doc_ids: int32 [6144], replicated, may hold values from 0 to 15, as said below
- image_flags: int32 [6144], replicated, may hold values from 0 to 1, as said below
- labels: int32 [6144], P(('seq', 'head')), may hold values from -1 to 31999, as said below
- token_loss: float32 [6144], P(('seq', 'head')), may hold values from 0.05 to 8
Outputs:
- attended: bfloat16 [6144, 4096], P(('seq', 'head'))
- doc_count: float32 [16], replicated
- doc_loss: float32 [16], replicated
Inputs may be any that keep to these rules, and one draw needn't show every extreme that they name: `doc_ids`: document numbers never fall along the sequence and rise by one from one document to the next; every document holds at least 64 and at most 704 tokens, and some document holds exactly 704. `image_flags`: the 1s form spans of exactly 576 consecutive tokens, at most one span a document, each inside one document and never at its first token. `labels`: every image token has -1, and some document has -1 on all of its tokens.
All inputs are finite; a program needn't handle non-finite values.
Results may differ from a plain program's by a relative error of at most 0.0034.
Values may be sent and summed in bfloat16 or wider, within the bound.
No kernel may reach another device: no remote copies, remote signals or barrier semaphores. Data moves between devices by JAX's collectives and lax.ppermute only.
A program may use at most 128 MiB of HBM per device.

v0:
```python
import jax
import jax.numpy as jnp
from jax import lax
from jax.sharding import PartitionSpec as P

HEAD_DIM = 128
TOK_DEV = 768
DOC_MEAN = 384
DOC_MOST = 704
IMG_LEN = 576


def shifted(block, axis, distance):
    devices = range(lax.axis_size(axis))
    route = [(i - distance, i) for i in devices if i - distance in devices]
    return lax.ppermute(block, axis, route)


def cut_rows(reach):
    return min(TOK_DEV, -(-reach // 128) * 128)


def allowed_pairs(query_docs, query_flags, query_places, key_docs, key_flags, key_places):
    same = query_docs[:, None] == key_docs[None, :]
    earlier = key_places[None, :] <= query_places[:, None]
    image = (query_flags[:, None] == 1) & (key_flags[None, :] == 1)
    return same & (earlier | image)


def attend(query_part, key_window, value_window, allowed):
    outputs = []
    scale = HEAD_DIM ** (-0.5)
    for head_index in range(query_part.shape[1] // HEAD_DIM):
        lower = head_index * HEAD_DIM
        query_head = query_part[:, lower : lower + HEAD_DIM]
        key_head = key_window[:, lower : lower + HEAD_DIM]
        value_head = value_window[:, lower : lower + HEAD_DIM]
        scores = (
            lax.dot_general(
                query_head, key_head, (((1,), (1,)), ((), ())), preferred_element_type=jnp.float32
            )
            * scale
        )
        scores = jnp.where(allowed, scores, -jnp.inf)
        row_max = jnp.max(scores, axis=1, keepdims=True)
        weights = jnp.exp(scores - row_max)
        total = jnp.sum(weights, axis=1, keepdims=True)
        mixed = (
            jnp.dot(weights.astype(jnp.bfloat16), value_head, preferred_element_type=jnp.float32)
            / total
        )
        outputs.append(mixed.astype(jnp.bfloat16))
    return jnp.concatenate(outputs, axis=1)


def per_device(queries, key_rows, values, doc_ids, image_flags, labels, token_loss):
    query_local, key_local, value_local = (
        lax.all_to_all(queries, "head", split_axis=1, concat_axis=0, tiled=True),
        lax.all_to_all(key_rows, "head", split_axis=1, concat_axis=0, tiled=True),
        lax.all_to_all(values, "head", split_axis=1, concat_axis=0, tiled=True),
    )
    reach_back = (DOC_MOST + TOK_DEV - 2) // TOK_DEV
    reach_front = (IMG_LEN + TOK_DEV - 2) // TOK_DEV
    behind = [shifted((key_local, value_local), "seq", 1)]
    ahead = [
        shifted(
            (
                key_local[: cut_rows(IMG_LEN - 1 - (1 - 1) * TOK_DEV)],
                value_local[: cut_rows(IMG_LEN - 1 - (1 - 1) * TOK_DEV)],
            ),
            "seq",
            -1,
        )
    ]
    key_window = jnp.concatenate(
        [pair[0] for pair in behind] + [key_local] + [pair[0] for pair in ahead], axis=0
    )
    value_window = jnp.concatenate(
        [pair[1] for pair in behind] + [value_local] + [pair[1] for pair in ahead], axis=0
    )
    back_total = sum((pair[0].shape[0] for pair in behind))
    window_rows = key_window.shape[0]
    block_start = lax.axis_index("seq") * TOK_DEV
    pad_front = reach_back * TOK_DEV
    pad_back = reach_front * TOK_DEV
    padded_docs = jnp.pad(doc_ids, (pad_front, pad_back), constant_values=-1)
    padded_flags = jnp.pad(image_flags, (pad_front, pad_back))
    key_docs = lax.dynamic_slice_in_dim(
        padded_docs, block_start + pad_front - back_total, window_rows
    )
    key_flags = lax.dynamic_slice_in_dim(
        padded_flags, block_start + pad_front - back_total, window_rows
    )
    query_docs = lax.dynamic_slice_in_dim(doc_ids, block_start, TOK_DEV)
    query_flags = lax.dynamic_slice_in_dim(image_flags, block_start, TOK_DEV)
    query_places = block_start + jnp.arange(TOK_DEV, dtype=jnp.int32)
    key_places = block_start - back_total + jnp.arange(window_rows, dtype=jnp.int32)
    allowed = allowed_pairs(query_docs, query_flags, query_places, key_docs, key_flags, key_places)
    attended = attend(query_local, key_window, value_window, allowed)
    output = lax.all_to_all(attended, "head", split_axis=0, concat_axis=1, tiled=True)
    local_rows = labels.shape[0]
    row_start = (
        lax.axis_index("seq") * lax.axis_size("head") + lax.axis_index("head")
    ) * local_rows
    local_docs = lax.dynamic_slice_in_dim(doc_ids, row_start, local_rows)
    documents = doc_ids.shape[0] // DOC_MEAN
    member = (local_docs[:, None] == jnp.arange(documents, dtype=jnp.int32)[None, :]) & (
        labels[:, None] >= 0
    )
    counts = jnp.sum(member.astype(jnp.float32), axis=0)
    sums = jnp.sum(jnp.where(member, token_loss[:, None], jnp.float32(0.0)), axis=0)
    counts, sums = lax.psum((counts, sums), ("seq", "head"))
    return (output, counts, sums / jnp.maximum(counts, jnp.float32(1.0)))


def solution(mesh):
    in_specs = (
        P(("seq", "head"), None),
        P(("seq", "head"), None),
        P(("seq", "head"), None),
        P(),
        P(),
        P(("seq", "head")),
        P(("seq", "head")),
    )
    out_specs = (P(("seq", "head"), None), P(), P())
    return jax.shard_map(
        per_device, mesh=mesh, in_specs=in_specs, out_specs=out_specs, check_vma=False
    )
```

profile of v0, /device:TPU:0, one launch (start us, length us, event | category | flops | bytes accessed | tf_op | source)
XLA Modules:
  0.0 272.2 jit_solution(8038829767457793462)
XLA Ops:
  0.6 2.8 %copy.36 = bf16[24,4,8,1024]{3,2,0,1:T(8,128)(2,1)} copy(bf16[24,4,8,1024]{3,2,1,0:T(8,128)(2,1)} %bitcast.54) | data formatting | bytes 3145728 | tf_op jit(solution)/shard_map/all_to_all | solution.py:59
  3.5 4.2 %all-to-all-start = ((bf16[192,4,1024]{2,0,1:T(8,128)(2,1)}), bf16[192,4,1024]{2,0,1:T(8,128)(2,1)S(1)}, u32[]{:S(2)}, u32[]{:S(2)}) async-start(bf16[192,4,1024]{2,0,1:T(8,128)(2,1)} %bitcast.40), calls=%async_computation | async-start | bytes 3145728 | tf_op jit(solution)/shard_map/all_to_all | solution.py:59
  9.0 18.7 %all-to-all-done = bf16[192,4,1024]{2,0,1:T(8,128)(2,1)S(1)} async-done(((bf16[192,4,1024]{2,0,1:T(8,128)(2,1)}), bf16[192,4,1024]{2,0,1:T(8,128)(2,1)S(1)}, u32[]{:S(2)}, u32[]{:S(2)}) %all-to-all-start) | async-done | bytes 1572896 | tf_op jit(solution)/shard_map/all_to_all | solution.py:59
  27.7 3.6 %all-to-all-start.2 = ((bf16[192,4,1024]{2,0,1:T(8,128)(2,1)}), bf16[192,4,1024]{2,0,1:T(8,128)(2,1)S(1)}, u32[]{:S(2)}, u32[]{:S(2)}) async-start(bf16[192,4,1024]{2,0,1:T(8,128)(2,1)} %bitcast.53), calls=%async_computation.2 | async-start | bytes 3145728 | tf_op jit(solution)/shard_map/all_to_all | solution.py:60
  31.3 5.4 %collective-permute-start = (bf16[768,1024]{1,0:T(8,128)(2,1)S(1)}, bf16[768,1024]{1,0:T(8,128)(2,1)}, u32[]{:S(2)}, u32[]{:S(2)}) collective-permute-start(bf16[768,1024]{1,0:T(8,128)(2,1)S(1)} %bitcast.44), channel_id=1, source_target_pairs={{0,4},{4,8},{8,12},{12,16},{16,20},{20,24},{24,28},{1,5},{5,9},{9,... | collective-permute-start | bytes 4718600 | tf_op jit(solution)/shard_map/ppermute | solution.py:16
  39.2 2.7 copy.35
  41.9 9.4 %all-to-all-done.2 = bf16[192,4,1024]{2,0,1:T(8,128)(2,1)S(1)} async-done(((bf16[192,4,1024]{2,0,1:T(8,128)(2,1)}), bf16[192,4,1024]{2,0,1:T(8,128)(2,1)S(1)}, u32[]{:S(2)}, u32[]{:S(2)}) %all-to-all-start.2) | async-done | bytes 1572896 | tf_op jit(solution)/shard_map/all_to_all | solution.py:60
  51.3 4.3 %all-to-all-start.1 = ((bf16[192,4,1024]{2,0,1:T(8,128)(2,1)}), bf16[192,4,1024]{2,0,1:T(8,128)(2,1)}, u32[]{:S(2)}, u32[]{:S(2)}) async-start(bf16[192,4,1024]{2,0,1:T(8,128)(2,1)} %bitcast.51), calls=%async_computation.1 | async-start | bytes 3145728 | tf_op jit(solution)/shard_map/all_to_all | solution.py:58
  57.2 5.3 %collective-permute-start.2 = (bf16[768,1024]{1,0:T(8,128)(2,1)S(1)}, bf16[768,1024]{1,0:T(8,128)(2,1)}, u32[]{:S(2)}, u32[]{:S(2)}) collective-permute-start(bf16[768,1024]{1,0:T(8,128)(2,1)S(1)} %bitcast.42), channel_id=1, source_target_pairs={{0,4},{4,8},{8,12},{12,16},{16,20},{20,24},{24,28},{1,5},{5,9},{9,... | collective-permute-start | bytes 4718600 | tf_op jit(solution)/shard_map/ppermute | solution.py:16
  63.9 7.9 %collective-permute-done.1 = bf16[640,1024]{1,0:T(8,128)(2,1)} collective-permute-done((bf16[640,1024]{1,0:T(8,128)(2,1)}, bf16[640,1024]{1,0:T(8,128)(2,1)}, u32[]{:S(2)}, u32[]{:S(2)}) %collective-permute-start.1) | collective-permute-done | bytes 1310752 | tf_op jit(solution)/shard_map/ppermute | solution.py:16
  71.8 54.7 %collective-permute-done = bf16[768,1024]{1,0:T(8,128)(2,1)} collective-permute-done((bf16[768,1024]{1,0:T(8,128)(2,1)S(1)}, bf16[768,1024]{1,0:T(8,128)(2,1)}, u32[]{:S(2)}, u32[]{:S(2)}) %collective-permute-start) | collective-permute-done | bytes 1572896 | tf_op jit(solution)/shard_map/ppermute | solution.py:16
  126.5 3.6 %pad_maximum_fusion = bf16[2176,1024]{1,0:T(8,128)(2,1)} fusion(bf16[640,1024]{1,0:T(8,128)(2,1)} %collective-permute-done.1, bf16[768,1024]{1,0:T(8,128)(2,1)S(1)} %bitcast.46, bf16[768,1024]{1,0:T(8,128)(2,1)} %collective-permute-done), kind=kLoop, calls=%fused_computation.33 | loop fusion | flops 13369344 | bytes 8912896 | tf_op jit(solution)/shard_map/concatenate | solution.py:75
  130.1 4.2 %fusion.138 = (f32[768]{0:T(1024)S(1)}, f32[768,2176]{0,1:T(8,128)S(1)}) fusion(bf16[768,1024]{1,0:T(8,128)(2,1)} %bitcast.4, bf16[2176,1024]{1,0:T(8,128)(2,1)} %pad_maximum_fusion, pred[2176]{0:T(1024)(128)(4,1)S(1)} %fusion.137, pred[768]{0:T(1024)(128)(4,1)S(1)} %dynamic-slice_compare_fusion, s32[768]{0:T(1024)S(1)} %iota_add_fusion.1, ...), kind=kOutput, calls=%fused_computation.114 | convolution fusion | flops 441187584 | bytes 7467904 | tf_op jit(solution)/shard_map/dot_general | solution.py:39
  134.4 6.3 %fusion.139 = (f32[768]{0:T(1024)S(1)}, f32[768,2176]{0,1:T(8,128)}) fusion(bf16[768,1024]{1,0:T(8,128)(2,1)} %bitcast.4, bf16[2176,1024]{1,0:T(8,128)(2,1)S(1)} %copy-done.1, pred[2176]{0:T(1024)(128)(4,1)S(1)} %fusion.137, pred[768]{0:T(1024)(128)(4,1)S(1)} %dynamic-slice_compare_fusion, s32[768]{0:T(1024)S(1)} %iota_add_fusion.1, ...), kind=kOutput, calls=%fused_computation.115 | convolution fusion | flops 441187584 | bytes 7478272 | tf_op jit(solution)/shard_map/dot_general | solution.py:39
  140.7 5.9 %fusion.140 = (f32[768]{0:T(1024)S(1)}, f32[768,2176]{0,1:T(8,128)}) fusion(bf16[768,1024]{1,0:T(8,128)(2,1)} %bitcast.4, bf16[2176,1024]{1,0:T(8,128)(2,1)S(1)} %copy-done.1, pred[2176]{0:T(1024)(128)(4,1)S(1)} %fusion.137, pred[768]{0:T(1024)(128)(4,1)S(1)} %dynamic-slice_compare_fusion, s32[768]{0:T(1024)S(1)} %iota_add_fusion.1, ...), kind=kOutput, calls=%fused_computation.116 | convolution fusion | flops 441187584 | bytes 7478272 | tf_op jit(solution)/shard_map/dot_general | solution.py:39
  146.6 6.0 %fusion.141 = (f32[768]{0:T(1024)S(1)}, f32[768,2176]{0,1:T(8,128)}) fusion(bf16[768,1024]{1,0:T(8,128)(2,1)} %bitcast.4, bf16[2176,1024]{1,0:T(8,128)(2,1)S(1)} %copy-done.1, pred[2176]{0:T(1024)(128)(4,1)S(1)} %fusion.137, pred[768]{0:T(1024)(128)(4,1)S(1)} %dynamic-slice_compare_fusion, s32[768]{0:T(1024)S(1)} %iota_add_fusion.1, ...), kind=kOutput, calls=%fused_computation.117 | convolution fusion | flops 441187584 | bytes 7478272 | tf_op jit(solution)/shard_map/dot_general | solution.py:39
  152.5 3.6 %fusion.142 = (f32[768]{0:T(1024)S(1)}, f32[768,2176]{0,1:T(8,128)S(1)}) fusion(bf16[768,1024]{1,0:T(8,128)(2,1)} %bitcast.4, bf16[2176,1024]{1,0:T(8,128)(2,1)S(1)} %copy-done.1, pred[2176]{0:T(1024)(128)(4,1)S(1)} %fusion.137, pred[768]{0:T(1024)(128)(4,1)S(1)} %dynamic-slice_compare_fusion, s32[768]{0:T(1024)S(1)} %iota_add_fusion.1, ...), kind=kOutput, calls=%fused_computation.118 | convolution fusion | flops 441187584 | bytes 7478272 | tf_op jit(solution)/shard_map/dot_general | solution.py:39
  156.2 3.6 %fusion.143 = (f32[768]{0:T(1024)S(1)}, f32[768,2176]{0,1:T(8,128)S(1)}) fusion(bf16[768,1024]{1,0:T(8,128)(2,1)} %bitcast.4, bf16[2176,1024]{1,0:T(8,128)(2,1)S(1)} %copy-done.1, pred[2176]{0:T(1024)(128)(4,1)S(1)} %fusion.137, pred[768]{0:T(1024)(128)(4,1)S(1)} %dynamic-slice_compare_fusion, s32[768]{0:T(1024)S(1)} %iota_add_fusion.1, ...), kind=kOutput, calls=%fused_computation.119 | convolution fusion | flops 441187584 | bytes 7478272 | tf_op jit(solution)/shard_map/dot_general | solution.py:39
  160.8 3.6 %fusion.144 = (f32[768]{0:T(1024)S(1)}, f32[768,2176]{0,1:T(8,128)S(1)}) fusion(bf16[768,1024]{1,0:T(8,128)(2,1)} %bitcast.4, bf16[2176,1024]{1,0:T(8,128)(2,1)S(1)} %copy-done.1, pred[2176]{0:T(1024)(128)(4,1)S(1)} %fusion.137, pred[768]{0:T(1024)(128)(4,1)S(1)} %dynamic-slice_compare_fusion, s32[768]{0:T(1024)S(1)} %iota_add_fusion.1, ...), kind=kOutput, calls=%fused_computation.120 | convolution fusion | flops 441187584 | bytes 7478272 | tf_op jit(solution)/shard_map/dot_general | solution.py:39
  164.5 3.9 %fusion.145 = (f32[768]{0:T(1024)S(1)}, f32[768,2176]{0,1:T(8,128)S(1)}) fusion(bf16[768,1024]{1,0:T(8,128)(2,1)} %bitcast.4, bf16[2176,1024]{1,0:T(8,128)(2,1)S(1)} %copy-done.1, pred[2176]{0:T(1024)(128)(4,1)S(1)} %fusion.137, pred[768]{0:T(1024)(128)(4,1)S(1)} %dynamic-slice_compare_fusion, s32[768]{0:T(1024)S(1)} %iota_add_fusion.1, ...), kind=kOutput, calls=%fused_computation.121 | convolution fusion | flops 441187584 | bytes 7478272 | tf_op jit(solution)/shard_map/dot_general | solution.py:39
  168.4 3.9 %pad_maximum_fusion.1 = bf16[2176,1024]{1,0:T(8,128)(2,1)} fusion(bf16[640,1024]{1,0:T(8,128)(2,1)} %collective-permute-done.3, bf16[768,1024]{1,0:T(8,128)(2,1)S(1)} %bitcast.43, bf16[768,1024]{1,0:T(8,128)(2,1)} %collective-permute-done.2), kind=kLoop, calls=%fused_computation.34 | loop fusion | flops 13369344 | bytes 8912896 | tf_op jit(solution)/shard_map/concatenate | solution.py:78
  172.2 4.3 %fusion.46 = bf16[768,1024]{0,1:T(8,128)(2,1)S(1)} fusion(f32[768,2176]{0,1:T(8,128)} %copy-done, f32[768]{0:T(1024)S(1)} %get-tuple-element.7, bf16[2176,1024]{1,0:T(8,128)(2,1)} %pad_maximum_fusion.1, f32[768]{0:T(1024)S(1)} %fusion), kind=kOutput, calls=%fused_computation.56 | convolution fusion | flops 431357952 | bytes 7444480 | tf_op jit(solution)/shard_map/dot_general | solution.py:49
  177.5 2.3 fusion.55
  179.8 4.0 %fusion.4 = f32[768]{0:T(1024)S(1)} fusion(f32[768,2176]{0,1:T(8,128)} %get-tuple-element.12, f32[768]{0:T(1024)S(1)} %get-tuple-element.11), kind=kLoop, calls=%fused_computation.21 | loop fusion | flops 3341568 | bytes 6690816 | tf_op jit(solution)/shard_map/reduce_sum | solution.py:47
  183.8 4.3 %fusion.64 = bf16[768,1024]{0,1:T(8,128)(2,1)S(1)} fusion(bf16[768,1024]{0,1:T(8,128)(2,1)S(1)} %fusion.55, f32[768,2176]{0,1:T(8,128)} %get-tuple-element.12, f32[768]{0:T(1024)S(1)} %get-tuple-element.11, bf16[2176,1024]{1,0:T(8,128)(2,1)} %pad_maximum_fusion.1, f32[768]{0:T(1024)S(1)} %fusion.4), kind=kOutput, calls=%fused_computation.62 | convolution fusion | flops 431357952 | bytes 7446528 | tf_op jit(solution)/shard_map/dot_general | solution.py:49
  189.1 2.3 fusion.73
  192.3 2.3 fusion.82
  195.5 2.3 fusion.91
  199.0 2.3 fusion.100
  202.3 2.3 fusion.109
  206.2 3.6 %all-to-all-start.3 = ((bf16[4,192,1024]{2,1,0:T(8,128)(2,1)}), bf16[4,192,1024]{2,1,0:T(8,128)(2,1)S(1)}, u32[]{:S(2)}, u32[]{:S(2)}) async-start(bf16[4,192,1024]{2,1,0:T(8,128)(2,1)} %bitcast.17), calls=%async_computation.3 | async-start | bytes 3145728 | tf_op jit(solution)/shard_map/all_to_all | solution.py:100
  210.0 60.4 %all-reduce.2 = (f32[16]{0:T(128)S(1)}, f32[16]{0:T(128)S(1)}) all-reduce(f32[16]{0:T(128)S(1)} %get-tuple-element.4, f32[16]{0:T(128)S(1)} %get-tuple-element.3), channel_id=1, replica_groups=mesh['seq'=8,'head'=4] {'seq','head'}, use_global_device_ids=true, to_apply=%region_17.18 | all-reduce | flops 32 | bytes 256 | tf_op jit(solution)/shard_map/psum | solution.py:112
  (54 shorter events, 17.2 us)
Async XLA Ops:
  0.6 7.1 %copy-start.2 = (bf16[192,4096]{1,0:T(8,128)(2,1)S(1)}, bf16[192,4096]{1,0:T(8,128)(2,1)}, u32[]{:S(2)}) copy-start(bf16[192,4096]{1,0:T(8,128)(2,1)} %param.9) | copy-start | bytes 4718596
  3.5 24.3 %all-to-all-start = ((bf16[192,4,1024]{2,0,1:T(8,128)(2,1)}), bf16[192,4,1024]{2,0,1:T(8,128)(2,1)S(1)}, u32[]{:S(2)}, u32[]{:S(2)}) async-start(bf16[192,4,1024]{2,0,1:T(8,128)(2,1)} %bitcast.40), calls=%async_computation | async-start | bytes 3145728 | tf_op jit(solution)/shard_map/all_to_all | solution.py:59
  27.7 23.6 %all-to-all-start.2 = ((bf16[192,4,1024]{2,0,1:T(8,128)(2,1)}), bf16[192,4,1024]{2,0,1:T(8,128)(2,1)S(1)}, u32[]{:S(2)}, u32[]{:S(2)}) async-start(bf16[192,4,1024]{2,0,1:T(8,128)(2,1)} %bitcast.53), calls=%async_computation.2 | async-start | bytes 3145728 | tf_op jit(solution)/shard_map/all_to_all | solution.py:60
  31.3 24.4 %copy-start.3 = (s32[6144]{0:T(1024)S(1)}, s32[6144]{0:T(1024)}, u32[]{:S(2)}) copy-start(s32[6144]{0:T(1024)} %param.10) | copy-start | bytes 73732
  31.3 24.5 %copy-start.4 = (s32[6144]{0:T(1024)S(1)}, s32[6144]{0:T(1024)}, u32[]{:S(2)}) copy-start(s32[6144]{0:T(1024)} %param.11) | copy-start | bytes 73732
  31.3 95.2 %collective-permute-start = (bf16[768,1024]{1,0:T(8,128)(2,1)S(1)}, bf16[768,1024]{1,0:T(8,128)(2,1)}, u32[]{:S(2)}, u32[]{:S(2)}) collective-permute-start(bf16[768,1024]{1,0:T(8,128)(2,1)S(1)} %bitcast.44), channel_id=1, source_target_pairs={{0,4},{4,8},{8,12},{12,16},{16,20},{20,24},{24,28},{1,5},{5,9},{9,... | collective-permute-start | bytes 4718600 | tf_op jit(solution)/shard_map/ppermute | solution.py:16
  37.9 33.8 %collective-permute-start.1 = (bf16[640,1024]{1,0:T(8,128)(2,1)}, bf16[640,1024]{1,0:T(8,128)(2,1)}, u32[]{:S(2)}, u32[]{:S(2)}) collective-permute-start(bf16[640,1024]{1,0:T(8,128)(2,1)} %slice.104), channel_id=1, source_target_pairs={{4,0},{8,4},{12,8},{16,12},{20,16},{24,20},{28,24},{5,1},{9,5},{13... | collective-permute-start | bytes 3932168 | tf_op jit(solution)/shard_map/ppermute | solution.py:16
  51.3 78.8 %all-to-all-start.1 = ((bf16[192,4,1024]{2,0,1:T(8,128)(2,1)}), bf16[192,4,1024]{2,0,1:T(8,128)(2,1)}, u32[]{:S(2)}, u32[]{:S(2)}) async-start(bf16[192,4,1024]{2,0,1:T(8,128)(2,1)} %bitcast.51), calls=%async_computation.1 | async-start | bytes 3145728 | tf_op jit(solution)/shard_map/all_to_all | solution.py:58
  57.2 111.1 %collective-permute-start.2 = (bf16[768,1024]{1,0:T(8,128)(2,1)S(1)}, bf16[768,1024]{1,0:T(8,128)(2,1)}, u32[]{:S(2)}, u32[]{:S(2)}) collective-permute-start(bf16[768,1024]{1,0:T(8,128)(2,1)S(1)} %bitcast.42), channel_id=1, source_target_pairs={{0,4},{4,8},{8,12},{12,16},{16,20},{20,24},{24,28},{1,5},{5,9},{9,... | collective-permute-start | bytes 4718600 | tf_op jit(solution)/shard_map/ppermute | solution.py:16
  62.6 105.8 %collective-permute-start.3 = (bf16[640,1024]{1,0:T(8,128)(2,1)}, bf16[640,1024]{1,0:T(8,128)(2,1)}, u32[]{:S(2)}, u32[]{:S(2)}) collective-permute-start(bf16[640,1024]{1,0:T(8,128)(2,1)} %slice.107), channel_id=1, source_target_pairs={{4,0},{8,4},{12,8},{16,12},{20,16},{24,20},{28,24},{5,1},{9,5},{13... | collective-permute-start | bytes 3932168 | tf_op jit(solution)/shard_map/ppermute | solution.py:16
  130.1 4.2 %copy-start.1 = (bf16[2176,1024]{1,0:T(8,128)(2,1)S(1)}, bf16[2176,1024]{1,0:T(8,128)(2,1)}, u32[]{:S(2)}) copy-start(bf16[2176,1024]{1,0:T(8,128)(2,1)} %pad_maximum_fusion) | copy-start | bytes 13369348
  134.4 25.5 %copy-start = (f32[768,2176]{0,1:T(8,128)}, f32[768,2176]{0,1:T(8,128)S(1)}, u32[]{:S(2)}) copy-start(f32[768,2176]{0,1:T(8,128)S(1)} %get-tuple-element.8) | copy-start | bytes 20054020
  168.3 8.2 %slice-start.2 = ((s8[6684672]{0:T(1024)(128)(4,1)}), s8[4194304]{0:T(1024)(128)(4,1)S(1)}, s32[]{:S(2)}) async-start(s8[6684672]{0:T(1024)(128)(4,1)} %bitcast.49), calls=%async_computation.6 | async-start | bytes 8388608
  172.2 4.3 %slice-start.3 = ((s8[6684672]{0:T(1024)(128)(4,1)}), s8[2490368]{0:T(1024)(128)(4,1)S(1)}, s32[]{:S(2)}) async-start(s8[6684672]{0:T(1024)(128)(4,1)} %bitcast.49), calls=%async_computation.7 | async-start | bytes 4980736
  179.8 8.3 %slice-start = ((s8[6684672]{0:T(1024)(128)(4,1)}), s8[4194304]{0:T(1024)(128)(4,1)S(1)}, s32[]{:S(2)}) async-start(s8[6684672]{0:T(1024)(128)(4,1)} %bitcast.47), calls=%async_computation.4 | async-start | bytes 8388608
  183.8 4.3 %slice-start.1 = ((s8[6684672]{0:T(1024)(128)(4,1)}), s8[2490368]{0:T(1024)(128)(4,1)S(1)}, s32[]{:S(2)}) async-start(s8[6684672]{0:T(1024)(128)(4,1)} %bitcast.47), calls=%async_computation.5 | async-start | bytes 4980736
  204.5 5.3 %copy-start.6 = (s32[192]{0:T(256)S(1)}, s32[192]{0:T(256)}, u32[]{:S(2)}) copy-start(s32[192]{0:T(256)} %param.12) | copy-start | bytes 2308
  204.5 5.3 %copy-start.5 = (f32[192]{0:T(256)S(1)}, f32[192]{0:T(256)}, u32[]{:S(2)}) copy-start(f32[192]{0:T(256)} %param.13) | copy-start | bytes 2308
  206.2 64.7 %all-to-all-start.3 = ((bf16[4,192,1024]{2,1,0:T(8,128)(2,1)}), bf16[4,192,1024]{2,1,0:T(8,128)(2,1)S(1)}, u32[]{:S(2)}, u32[]{:S(2)}) async-start(bf16[4,192,1024]{2,1,0:T(8,128)(2,1)} %bitcast.17), calls=%async_computation.3 | async-start | bytes 3145728 | tf_op jit(solution)/shard_map/all_to_all | solution.py:100
  270.3 1.8 copy-start.7
where the time goes:
time: 273 us; the launch traced here: 272 us
  waiting for transfers between devices  90.8 us (33%)
  blocking collectives  60.4 us (22%)
  matrix products  59.3 us (22%)
  starting transfers between devices  29 us (11%)
  other arithmetic  19.2 us (7%)
  local copies, waits for them, and re-layouts  12.4 us (5%)
    ppermute x4, waiting for transfers between devices, shifted(): return lax.ppermute(block, axis, route)  62.6 us
    psum x1, blocking collectives, per_device(): counts, sums = lax.psum((counts, sums), ('seq', 'head'))  60.4 us
    dot_general x8, matrix products, attend(): lax.dot_general(query_head, key_head, (((1,), (1,)), ((), ())), preferred...  37.1 us
    dot_general x8, matrix products, attend(): jnp.dot(weights.astype(jnp.bfloat16), value_head, preferred_element_type=...  22.2 us
    all_to_all x1, waiting for transfers between devices, per_device(): lax.all_to_all(key_rows, 'head', split_axis=1, concat_axis=0, tiled=True)  18.7 us
    ppermute x4, starting transfers between devices, shifted(): return lax.ppermute(block, axis, route)  13.3 us
    reduce_sum x8, other arithmetic, attend(): total = jnp.sum(weights, axis=1, keepdims=True)  10.9 us
    all_to_all x1, waiting for transfers between devices, per_device(): lax.all_to_all(values, 'head', split_axis=1, concat_axis=0, tiled=True)  9.44 us
  transfers between devices with their start and end apart: 8, of which 4 were waited for; matrix products, arithmetic and copies ran while one was open for 18% of the time, Pallas kernels for 0%

commit v1 on v0

--- a/solution.py
+++ b/solution.py
@@ -8,6 +8,13 @@
 DOC_MEAN = 384
 DOC_MOST = 704
 IMG_LEN = 576
+
+
+def swap_blocks(array, name, split, join):
+    peers = lax.axis_size(name)
+    parts = jnp.stack(jnp.split(array, peers, axis=split), axis=0)
+    parts = lax.all_to_all(parts, name, split_axis=0, concat_axis=0)
+    return jnp.concatenate(parts, axis=join)
 
 
 def shifted(block, axis, distance):
@@ -56,7 +63,7 @@
 def per_device(queries, key_rows, values, doc_ids, image_flags, labels, token_loss):
     query_local, key_local, value_local = (
         lax.all_to_all(queries, "head", split_axis=1, concat_axis=0, tiled=True),
-        lax.all_to_all(key_rows, "head", split_axis=1, concat_axis=0, tiled=True),
+        swap_blocks(key_rows, "head", 1, 0),
         lax.all_to_all(values, "head", split_axis=1, concat_axis=0, tiled=True),
     )
     reach_back = (DOC_MOST + TOK_DEV - 2) // TOK_DEV

time: 273 us -> 273 us (level)
    all_to_all x1 -> x0, local copies, waits for them, and re-layouts: 2.82 us -> none  [per_device(): lax.all_to_all(key_rows, 'head', split_axis=1, concat_axis=0, tiled=True)]
where the time goes in v1:
time: 273 us; the launch traced here: 272 us
  waiting for transfers between devices  90.8 us (33%)
  blocking collectives  60.4 us (22%)
  matrix products  59.3 us (22%)
  starting transfers between devices  29 us (11%)
  other arithmetic  20.6 us (8%)
  local copies, waits for them, and re-layouts  11.2 us (4%)
    ppermute x4, waiting for transfers between devices, shifted(): return lax.ppermute(block, axis, route)  62.6 us
    psum x1, blocking collectives, per_device(): counts, sums = lax.psum((counts, sums), ('seq', 'head'))  60.4 us
    dot_general x8, matrix products, attend(): lax.dot_general(query_head, key_head, (((1,), (1,)), ((), ())), preferred...  37.2 us
    dot_general x8, matrix products, attend(): jnp.dot(weights.astype(jnp.bfloat16), value_head, preferred_element_type=...  22.2 us
    all_to_all x1, waiting for transfers between devices, swap_blocks(): parts = lax.all_to_all(parts, name, split_axis=0, concat_axis=0)  18.7 us
    ppermute x4, starting transfers between devices, shifted(): return lax.ppermute(block, axis, route)  13.3 us
    reduce_sum x8, other arithmetic, attend(): total = jnp.sum(weights, axis=1, keepdims=True)  10.9 us
    all_to_all x1, waiting for transfers between devices, per_device(): lax.all_to_all(values, 'head', split_axis=1, concat_axis=0, tiled=True)  9.44 us
  transfers between devices with their start and end apart: 8, of which 4 were waited for; matrix products, arithmetic and copies ran while one was open for 18% of the time, Pallas kernels for 0%

profile of v1, /device:TPU:0, one launch (start us, length us, event | category | flops | bytes accessed | tf_op | source)
XLA Modules:
  0.0 272.3 jit_solution(2636868037146751547)
XLA Ops:
  3.6 4.2 %all-to-all-start = ((bf16[4,192,1024]{2,1,0:T(8,128)(2,1)}), bf16[4,192,1024]{2,1,0:T(8,128)(2,1)S(1)}, u32[]{:S(2)}, u32[]{:S(2)}) async-start(bf16[4,192,1024]{2,1,0:T(8,128)(2,1)} %pad_maximum_fusion.2), calls=%async_computation | async-start | bytes 3145728 | tf_op jit(solution)/shard_map/all_to_all | solution.py:16
  9.2 18.7 %all-to-all-done = bf16[4,192,1024]{2,1,0:T(8,128)(2,1)S(1)} async-done(((bf16[4,192,1024]{2,1,0:T(8,128)(2,1)}), bf16[4,192,1024]{2,1,0:T(8,128)(2,1)S(1)}, u32[]{:S(2)}, u32[]{:S(2)}) %all-to-all-start) | async-done | bytes 1572896 | tf_op jit(solution)/shard_map/all_to_all | solution.py:16
  27.9 3.6 %all-to-all-start.2 = ((bf16[192,4,1024]{2,0,1:T(8,128)(2,1)}), bf16[192,4,1024]{2,0,1:T(8,128)(2,1)S(1)}, u32[]{:S(2)}, u32[]{:S(2)}) async-start(bf16[192,4,1024]{2,0,1:T(8,128)(2,1)} %bitcast.55), calls=%async_computation.2 | async-start | bytes 3145728 | tf_op jit(solution)/shard_map/all_to_all | solution.py:67
  31.5 5.4 %collective-permute-start = (bf16[768,1024]{1,0:T(8,128)(2,1)S(1)}, bf16[768,1024]{1,0:T(8,128)(2,1)}, u32[]{:S(2)}, u32[]{:S(2)}) collective-permute-start(bf16[768,1024]{1,0:T(8,128)(2,1)S(1)} %bitcast.46), channel_id=1, source_target_pairs={{0,4},{4,8},{8,12},{12,16},{16,20},{20,24},{24,28},{1,5},{5,9},{9,... | collective-permute-start | bytes 4718600 | tf_op jit(solution)/shard_map/ppermute | solution.py:23
  39.3 2.7 copy.30
  42.0 9.4 %all-to-all-done.2 = bf16[192,4,1024]{2,0,1:T(8,128)(2,1)S(1)} async-done(((bf16[192,4,1024]{2,0,1:T(8,128)(2,1)}), bf16[192,4,1024]{2,0,1:T(8,128)(2,1)S(1)}, u32[]{:S(2)}, u32[]{:S(2)}) %all-to-all-start.2) | async-done | bytes 1572896 | tf_op jit(solution)/shard_map/all_to_all | solution.py:67
  51.5 4.3 %all-to-all-start.1 = ((bf16[192,4,1024]{2,0,1:T(8,128)(2,1)}), bf16[192,4,1024]{2,0,1:T(8,128)(2,1)}, u32[]{:S(2)}, u32[]{:S(2)}) async-start(bf16[192,4,1024]{2,0,1:T(8,128)(2,1)} %bitcast.53), calls=%async_computation.1 | async-start | bytes 3145728 | tf_op jit(solution)/shard_map/all_to_all | solution.py:65
  57.4 5.3 %collective-permute-start.2 = (bf16[768,1024]{1,0:T(8,128)(2,1)S(1)}, bf16[768,1024]{1,0:T(8,128)(2,1)}, u32[]{:S(2)}, u32[]{:S(2)}) collective-permute-start(bf16[768,1024]{1,0:T(8,128)(2,1)S(1)} %bitcast.44), channel_id=1, source_target_pairs={{0,4},{4,8},{8,12},{12,16},{16,20},{20,24},{24,28},{1,5},{5,9},{9,... | collective-permute-start | bytes 4718600 | tf_op jit(solution)/shard_map/ppermute | solution.py:23
  64.0 7.9 %collective-permute-done.1 = bf16[640,1024]{1,0:T(8,128)(2,1)} collective-permute-done((bf16[640,1024]{1,0:T(8,128)(2,1)}, bf16[640,1024]{1,0:T(8,128)(2,1)}, u32[]{:S(2)}, u32[]{:S(2)}) %collective-permute-start.1) | collective-permute-done | bytes 1310752 | tf_op jit(solution)/shard_map/ppermute | solution.py:23
  71.9 54.7 %collective-permute-done = bf16[768,1024]{1,0:T(8,128)(2,1)} collective-permute-done((bf16[768,1024]{1,0:T(8,128)(2,1)S(1)}, bf16[768,1024]{1,0:T(8,128)(2,1)}, u32[]{:S(2)}, u32[]{:S(2)}) %collective-permute-start) | collective-permute-done | bytes 1572896 | tf_op jit(solution)/shard_map/ppermute | solution.py:23
  126.6 3.6 %pad_maximum_fusion = bf16[2176,1024]{1,0:T(8,128)(2,1)} fusion(bf16[640,1024]{1,0:T(8,128)(2,1)} %collective-permute-done.1, bf16[768,1024]{1,0:T(8,128)(2,1)S(1)} %bitcast.48, bf16[768,1024]{1,0:T(8,128)(2,1)} %collective-permute-done), kind=kLoop, calls=%fused_computation.33 | loop fusion | flops 13369344 | bytes 8912896 | tf_op jit(solution)/shard_map/concatenate | solution.py:82
  130.3 4.2 %fusion.138 = (f32[768]{0:T(1024)S(1)}, f32[768,2176]{0,1:T(8,128)S(1)}) fusion(bf16[768,1024]{1,0:T(8,128)(2,1)} %bitcast.6, bf16[2176,1024]{1,0:T(8,128)(2,1)} %pad_maximum_fusion, pred[2176]{0:T(1024)(128)(4,1)S(1)} %fusion.137, pred[768]{0:T(1024)(128)(4,1)S(1)} %dynamic-slice_compare_fusion, s32[768]{0:T(1024)S(1)} %iota_add_fusion.1, ...), kind=kOutput, calls=%fused_computation.118 | convolution fusion | flops 441187584 | bytes 7467904 | tf_op jit(solution)/shard_map/dot_general | solution.py:46
  134.6 6.3 %fusion.139 = (f32[768]{0:T(1024)S(1)}, f32[768,2176]{0,1:T(8,128)}) fusion(bf16[768,1024]{1,0:T(8,128)(2,1)} %bitcast.6, bf16[2176,1024]{1,0:T(8,128)(2,1)S(1)} %copy-done.1, pred[2176]{0:T(1024)(128)(4,1)S(1)} %fusion.137, pred[768]{0:T(1024)(128)(4,1)S(1)} %dynamic-slice_compare_fusion, s32[768]{0:T(1024)S(1)} %iota_add_fusion.1, ...), kind=kOutput, calls=%fused_computation.119 | convolution fusion | flops 441187584 | bytes 7478272 | tf_op jit(solution)/shard_map/dot_general | solution.py:46
  140.8 5.9 %fusion.140 = (f32[768]{0:T(1024)S(1)}, f32[768,2176]{0,1:T(8,128)}) fusion(bf16[768,1024]{1,0:T(8,128)(2,1)} %bitcast.6, bf16[2176,1024]{1,0:T(8,128)(2,1)S(1)} %copy-done.1, pred[2176]{0:T(1024)(128)(4,1)S(1)} %fusion.137, pred[768]{0:T(1024)(128)(4,1)S(1)} %dynamic-slice_compare_fusion, s32[768]{0:T(1024)S(1)} %iota_add_fusion.1, ...), kind=kOutput, calls=%fused_computation.120 | convolution fusion | flops 441187584 | bytes 7478272 | tf_op jit(solution)/shard_map/dot_general | solution.py:46
  146.7 6.0 %fusion.141 = (f32[768]{0:T(1024)S(1)}, f32[768,2176]{0,1:T(8,128)}) fusion(bf16[768,1024]{1,0:T(8,128)(2,1)} %bitcast.6, bf16[2176,1024]{1,0:T(8,128)(2,1)S(1)} %copy-done.1, pred[2176]{0:T(1024)(128)(4,1)S(1)} %fusion.137, pred[768]{0:T(1024)(128)(4,1)S(1)} %dynamic-slice_compare_fusion, s32[768]{0:T(1024)S(1)} %iota_add_fusion.1, ...), kind=kOutput, calls=%fused_computation.121 | convolution fusion | flops 441187584 | bytes 7478272 | tf_op jit(solution)/shard_map/dot_general | solution.py:46
  152.7 3.6 %fusion.142 = (f32[768]{0:T(1024)S(1)}, f32[768,2176]{0,1:T(8,128)S(1)}) fusion(bf16[768,1024]{1,0:T(8,128)(2,1)} %bitcast.6, bf16[2176,1024]{1,0:T(8,128)(2,1)S(1)} %copy-done.1, pred[2176]{0:T(1024)(128)(4,1)S(1)} %fusion.137, pred[768]{0:T(1024)(128)(4,1)S(1)} %dynamic-slice_compare_fusion, s32[768]{0:T(1024)S(1)} %iota_add_fusion.1, ...), kind=kOutput, calls=%fused_computation.122 | convolution fusion | flops 441187584 | bytes 7478272 | tf_op jit(solution)/shard_map/dot_general | solution.py:46
  156.3 3.6 %fusion.143 = (f32[768]{0:T(1024)S(1)}, f32[768,2176]{0,1:T(8,128)S(1)}) fusion(bf16[768,1024]{1,0:T(8,128)(2,1)} %bitcast.6, bf16[2176,1024]{1,0:T(8,128)(2,1)S(1)} %copy-done.1, pred[2176]{0:T(1024)(128)(4,1)S(1)} %fusion.137, pred[768]{0:T(1024)(128)(4,1)S(1)} %dynamic-slice_compare_fusion, s32[768]{0:T(1024)S(1)} %iota_add_fusion.1, ...), kind=kOutput, calls=%fused_computation.123 | convolution fusion | flops 441187584 | bytes 7478272 | tf_op jit(solution)/shard_map/dot_general | solution.py:46
  161.0 3.6 %fusion.144 = (f32[768]{0:T(1024)S(1)}, f32[768,2176]{0,1:T(8,128)S(1)}) fusion(bf16[768,1024]{1,0:T(8,128)(2,1)} %bitcast.6, bf16[2176,1024]{1,0:T(8,128)(2,1)S(1)} %copy-done.1, pred[2176]{0:T(1024)(128)(4,1)S(1)} %fusion.137, pred[768]{0:T(1024)(128)(4,1)S(1)} %dynamic-slice_compare_fusion, s32[768]{0:T(1024)S(1)} %iota_add_fusion.1, ...), kind=kOutput, calls=%fused_computation.124 | convolution fusion | flops 441187584 | bytes 7478272 | tf_op jit(solution)/shard_map/dot_general | solution.py:46
  164.6 3.9 %fusion.145 = (f32[768]{0:T(1024)S(1)}, f32[768,2176]{0,1:T(8,128)S(1)}) fusion(bf16[768,1024]{1,0:T(8,128)(2,1)} %bitcast.6, bf16[2176,1024]{1,0:T(8,128)(2,1)S(1)} %copy-done.1, pred[2176]{0:T(1024)(128)(4,1)S(1)} %fusion.137, pred[768]{0:T(1024)(128)(4,1)S(1)} %dynamic-slice_compare_fusion, s32[768]{0:T(1024)S(1)} %iota_add_fusion.1, ...), kind=kOutput, calls=%fused_computation.125 | convolution fusion | flops 441187584 | bytes 7478272 | tf_op jit(solution)/shard_map/dot_general | solution.py:46
  168.5 3.9 %pad_maximum_fusion.1 = bf16[2176,1024]{1,0:T(8,128)(2,1)} fusion(bf16[640,1024]{1,0:T(8,128)(2,1)} %collective-permute-done.3, bf16[768,1024]{1,0:T(8,128)(2,1)S(1)} %bitcast.45, bf16[768,1024]{1,0:T(8,128)(2,1)} %collective-permute-done.2), kind=kLoop, calls=%fused_computation.34 | loop fusion | flops 13369344 | bytes 8912896 | tf_op jit(solution)/shard_map/concatenate | solution.py:85
  172.4 4.3 %fusion.46 = bf16[768,1024]{0,1:T(8,128)(2,1)S(1)} fusion(f32[768,2176]{0,1:T(8,128)} %copy-done, f32[768]{0:T(1024)S(1)} %get-tuple-element.11, bf16[2176,1024]{1,0:T(8,128)(2,1)} %pad_maximum_fusion.1, f32[768]{0:T(1024)S(1)} %fusion), kind=kOutput, calls=%fused_computation.56 | convolution fusion | flops 431357952 | bytes 7444480 | tf_op jit(solution)/shard_map/dot_general | solution.py:56
  177.7 2.3 fusion.55
  180.0 4.0 %fusion.4 = f32[768]{0:T(1024)S(1)} fusion(f32[768,2176]{0,1:T(8,128)} %get-tuple-element.16, f32[768]{0:T(1024)S(1)} %get-tuple-element.15), kind=kLoop, calls=%fused_computation.21 | loop fusion | flops 3341568 | bytes 6690816 | tf_op jit(solution)/shard_map/reduce_sum | solution.py:54
  184.0 4.3 %fusion.64 = bf16[768,1024]{0,1:T(8,128)(2,1)S(1)} fusion(bf16[768,1024]{0,1:T(8,128)(2,1)S(1)} %fusion.55, f32[768,2176]{0,1:T(8,128)} %get-tuple-element.16, f32[768]{0:T(1024)S(1)} %get-tuple-element.15, bf16[2176,1024]{1,0:T(8,128)(2,1)} %pad_maximum_fusion.1, f32[768]{0:T(1024)S(1)} %fusion.4), kind=kOutput, calls=%fused_computation.62 | convolution fusion | flops 431357952 | bytes 7446528 | tf_op jit(solution)/shard_map/dot_general | solution.py:56
  189.3 2.3 fusion.73
  192.5 2.3 fusion.82
  195.7 2.3 fusion.91
  199.2 2.3 fusion.100
  202.4 2.3 fusion.109
  204.7 1.6 copy.22
  206.3 3.6 %all-to-all-start.3 = ((bf16[4,192,1024]{2,1,0:T(8,128)(2,1)}), bf16[4,192,1024]{2,1,0:T(8,128)(2,1)S(1)}, u32[]{:S(2)}, u32[]{:S(2)}) async-start(bf16[4,192,1024]{2,1,0:T(8,128)(2,1)} %bitcast.19), calls=%async_computation.3 | async-start | bytes 3145728 | tf_op jit(solution)/shard_map/all_to_all | solution.py:107
  210.1 60.4 %all-reduce.2 = (f32[16]{0:T(128)S(1)}, f32[16]{0:T(128)S(1)}) all-reduce(f32[16]{0:T(128)S(1)} %get-tuple-element.4, f32[16]{0:T(128)S(1)} %get-tuple-element.3), channel_id=1, replica_groups=mesh['seq'=8,'head'=4] {'seq','head'}, use_global_device_ids=true, to_apply=%region_17.18 | all-reduce | flops 32 | bytes 256 | tf_op jit(solution)/shard_map/psum | solution.py:119
  (55 shorter events, 18.5 us)
Async XLA Ops:
  0.6 7.2 %copy-start.2 = (bf16[192,4096]{1,0:T(8,128)(2,1)S(1)}, bf16[192,4096]{1,0:T(8,128)(2,1)}, u32[]{:S(2)}) copy-start(bf16[192,4096]{1,0:T(8,128)(2,1)} %param.9) | copy-start | bytes 4718596
  3.6 24.3 %all-to-all-start = ((bf16[4,192,1024]{2,1,0:T(8,128)(2,1)}), bf16[4,192,1024]{2,1,0:T(8,128)(2,1)S(1)}, u32[]{:S(2)}, u32[]{:S(2)}) async-start(bf16[4,192,1024]{2,1,0:T(8,128)(2,1)} %pad_maximum_fusion.2), calls=%async_computation | async-start | bytes 3145728 | tf_op jit(solution)/shard_map/all_to_all | solution.py:16
  27.9 23.6 %all-to-all-start.2 = ((bf16[192,4,1024]{2,0,1:T(8,128)(2,1)}), bf16[192,4,1024]{2,0,1:T(8,128)(2,1)S(1)}, u32[]{:S(2)}, u32[]{:S(2)}) async-start(bf16[192,4,1024]{2,0,1:T(8,128)(2,1)} %bitcast.55), calls=%async_computation.2 | async-start | bytes 3145728 | tf_op jit(solution)/shard_map/all_to_all | solution.py:67
  31.5 24.4 %copy-start.3 = (s32[6144]{0:T(1024)S(1)}, s32[6144]{0:T(1024)}, u32[]{:S(2)}) copy-start(s32[6144]{0:T(1024)} %param.10) | copy-start | bytes 73732
  31.5 24.5 %copy-start.4 = (s32[6144]{0:T(1024)S(1)}, s32[6144]{0:T(1024)}, u32[]{:S(2)}) copy-start(s32[6144]{0:T(1024)} %param.11) | copy-start | bytes 73732
  31.5 95.2 %collective-permute-start = (bf16[768,1024]{1,0:T(8,128)(2,1)S(1)}, bf16[768,1024]{1,0:T(8,128)(2,1)}, u32[]{:S(2)}, u32[]{:S(2)}) collective-permute-start(bf16[768,1024]{1,0:T(8,128)(2,1)S(1)} %bitcast.46), channel_id=1, source_target_pairs={{0,4},{4,8},{8,12},{12,16},{16,20},{20,24},{24,28},{1,5},{5,9},{9,... | collective-permute-start | bytes 4718600 | tf_op jit(solution)/shard_map/ppermute | solution.py:23
  38.1 33.8 %collective-permute-start.1 = (bf16[640,1024]{1,0:T(8,128)(2,1)}, bf16[640,1024]{1,0:T(8,128)(2,1)}, u32[]{:S(2)}, u32[]{:S(2)}) collective-permute-start(bf16[640,1024]{1,0:T(8,128)(2,1)} %slice.104), channel_id=1, source_target_pairs={{4,0},{8,4},{12,8},{16,12},{20,16},{24,20},{28,24},{5,1},{9,5},{13... | collective-permute-start | bytes 3932168 | tf_op jit(solution)/shard_map/ppermute | solution.py:23
  51.5 78.8 %all-to-all-start.1 = ((bf16[192,4,1024]{2,0,1:T(8,128)(2,1)}), bf16[192,4,1024]{2,0,1:T(8,128)(2,1)}, u32[]{:S(2)}, u32[]{:S(2)}) async-start(bf16[192,4,1024]{2,0,1:T(8,128)(2,1)} %bitcast.53), calls=%async_computation.1 | async-start | bytes 3145728 | tf_op jit(solution)/shard_map/all_to_all | solution.py:65
  57.4 111.1 %collective-permute-start.2 = (bf16[768,1024]{1,0:T(8,128)(2,1)S(1)}, bf16[768,1024]{1,0:T(8,128)(2,1)}, u32[]{:S(2)}, u32[]{:S(2)}) collective-permute-start(bf16[768,1024]{1,0:T(8,128)(2,1)S(1)} %bitcast.44), channel_id=1, source_target_pairs={{0,4},{4,8},{8,12},{12,16},{16,20},{20,24},{24,28},{1,5},{5,9},{9,... | collective-permute-start | bytes 4718600 | tf_op jit(solution)/shard_map/ppermute | solution.py:23
  62.7 105.8 %collective-permute-start.3 = (bf16[640,1024]{1,0:T(8,128)(2,1)}, bf16[640,1024]{1,0:T(8,128)(2,1)}, u32[]{:S(2)}, u32[]{:S(2)}) collective-permute-start(bf16[640,1024]{1,0:T(8,128)(2,1)} %slice.107), channel_id=1, source_target_pairs={{4,0},{8,4},{12,8},{16,12},{20,16},{24,20},{28,24},{5,1},{9,5},{13... | collective-permute-start | bytes 3932168 | tf_op jit(solution)/shard_map/ppermute | solution.py:23
  130.3 4.2 %copy-start.1 = (bf16[2176,1024]{1,0:T(8,128)(2,1)S(1)}, bf16[2176,1024]{1,0:T(8,128)(2,1)}, u32[]{:S(2)}) copy-start(bf16[2176,1024]{1,0:T(8,128)(2,1)} %pad_maximum_fusion) | copy-start | bytes 13369348
  134.5 25.5 %copy-start = (f32[768,2176]{0,1:T(8,128)}, f32[768,2176]{0,1:T(8,128)S(1)}, u32[]{:S(2)}) copy-start(f32[768,2176]{0,1:T(8,128)S(1)} %get-tuple-element.12) | copy-start | bytes 20054020
  168.5 8.2 %slice-start.2 = ((s8[6684672]{0:T(1024)(128)(4,1)}), s8[4194304]{0:T(1024)(128)(4,1)S(1)}, s32[]{:S(2)}) async-start(s8[6684672]{0:T(1024)(128)(4,1)} %bitcast.51), calls=%async_computation.6 | async-start | bytes 8388608
  172.4 4.3 %slice-start.3 = ((s8[6684672]{0:T(1024)(128)(4,1)}), s8[2490368]{0:T(1024)(128)(4,1)S(1)}, s32[]{:S(2)}) async-start(s8[6684672]{0:T(1024)(128)(4,1)} %bitcast.51), calls=%async_computation.7 | async-start | bytes 4980736
  180.0 8.3 %slice-start = ((s8[6684672]{0:T(1024)(128)(4,1)}), s8[4194304]{0:T(1024)(128)(4,1)S(1)}, s32[]{:S(2)}) async-start(s8[6684672]{0:T(1024)(128)(4,1)} %bitcast.49), calls=%async_computation.4 | async-start | bytes 8388608
  184.0 4.3 %slice-start.1 = ((s8[6684672]{0:T(1024)(128)(4,1)}), s8[2490368]{0:T(1024)(128)(4,1)S(1)}, s32[]{:S(2)}) async-start(s8[6684672]{0:T(1024)(128)(4,1)} %bitcast.49), calls=%async_computation.5 | async-start | bytes 4980736
  204.7 5.3 %copy-start.6 = (s32[192]{0:T(256)S(1)}, s32[192]{0:T(256)}, u32[]{:S(2)}) copy-start(s32[192]{0:T(256)} %param.12) | copy-start | bytes 2308
  204.7 5.3 %copy-start.5 = (f32[192]{0:T(256)S(1)}, f32[192]{0:T(256)}, u32[]{:S(2)}) copy-start(f32[192]{0:T(256)} %param.13) | copy-start | bytes 2308
  206.3 64.7 %all-to-all-start.3 = ((bf16[4,192,1024]{2,1,0:T(8,128)(2,1)}), bf16[4,192,1024]{2,1,0:T(8,128)(2,1)S(1)}, u32[]{:S(2)}, u32[]{:S(2)}) async-start(bf16[4,192,1024]{2,1,0:T(8,128)(2,1)} %bitcast.19), calls=%async_computation.3 | async-start | bytes 3145728 | tf_op jit(solution)/shard_map/all_to_all | solution.py:107
  270.5 1.8 copy-start.7
